TPU v7x, 32 devices: a whole 2x2x4 slice. The times are simulated.
32 devices in a mesh: dp: 8 (over z, y), tensor: 4 (over x, core).
Axes of the slice: x: 2, y: 2, z: 4, core: 2. Of those that a mesh axis runs over, the one named last changes fastest.
Arguments:
- patches: bfloat16 [8192, 1280], P('dp'), may hold values from -27 to 27
- norm_gain: float32 [1280], replicated, may hold values from 0.1 to 1.9
- norm_bias: float32 [1280], replicated, may hold values from -3 to 3
- first_weight: bfloat16 [5120, 5120], P(None, 'tensor'), may hold values from -0.078125 to 0.078125
- first_bias: float32 [5120], P('tensor'), may hold values from -3 to 3
- second_weight: bfloat16 [5120, 8192], P('tensor', 'dp'), may hold values from -0.078125 to 0.078125
- second_bias: float32 [8192], P('tensor'), may hold values from -2 to 2
- text_embeds: bfloat16 [4096, 8192], P('dp', 'tensor'), may hold values from -36 to 36
- final_gain: float32 [8192], P('tensor'), may hold values from 0.1 to 1.9
- image_grids: int32 [8, 4, 2], replicated, may hold values from 2 to 8, as said below
- routing: int32 [8, 4], replicated, may hold values from 0 to 3, each once within a row
Outputs:
- embeddings: bfloat16 [4096, 8192], P('dp', 'tensor')
- normed: bfloat16 [4096, 8192], P('dp', 'tensor')
Inputs may be any that keep to these rules, and one draw needn't show every extreme that they name: `image_grids`: each image is a grid of 3 to 8 rows by 2 to 8 columns of merged tokens; in every draw some image is 8 by 8. `routing`: each row names every offset 0 to 3 once.
All inputs are finite; a program needn't handle non-finite values.
Results may differ from a plain program's by a relative error of at most 0.006.
Values may be sent and summed in bfloat16 or wider, within the bound.
A program may use at most 128 MiB of HBM per device.

v0:
```python
import jax
import jax.numpy as jnp
from jax import lax
from jax.sharding import PartitionSpec as P

D = 8192


def passed_along(block, axis, distance):
    devices = range(lax.axis_size(axis))
    route = [((i - distance) % len(devices), i) for i in devices]
    return lax.ppermute(block, axis, route)


def per_device(
    patches,
    norm_gain,
    norm_bias,
    first_weight,
    first_bias,
    second_weight,
    second_bias,
    text_embeds,
    final_gain,
    image_grids,
    routing,
):
    patch_values = patches.astype(jnp.float32)
    centered = patch_values - jnp.mean(patch_values, axis=-1, keepdims=True)
    variance = jnp.mean(centered * centered, axis=-1, keepdims=True)
    normed_patches = centered * lax.rsqrt(variance + 1e-06) * norm_gain + norm_bias
    merged = normed_patches.reshape(-1, first_weight.shape[0]).astype(jnp.bfloat16)
    hidden = jax.nn.gelu(
        jnp.dot(merged, first_weight, preferred_element_type=jnp.float32) + first_bias,
        approximate=False,
    ).astype(jnp.bfloat16)
    own_index = lax.axis_index("dp")
    shard_count = lax.axis_size("dp")
    partial_value = jnp.dot(
        lax.all_gather(hidden, "dp", axis=0, tiled=True),
        second_weight,
        preferred_element_type=jnp.float32,
    ).astype(jnp.bfloat16)
    columns = lax.all_to_all(partial_value, "dp", split_axis=0, concat_axis=1, tiled=True)
    partial_terms = columns.astype(jnp.float32)
    summed = lax.psum_scatter(
        partial_terms.astype(jnp.bfloat16), "tensor", scatter_dimension=1, tiled=True
    ).astype(jnp.float32)
    projected = (summed + second_bias).astype(jnp.bfloat16)
    block_total = image_grids.shape[1]
    cap_rows = projected.shape[0] // block_total
    feature_width = projected.shape[1]
    block_rows = projected.reshape(block_total, cap_rows, feature_width)
    counts_all = image_grids[:, :, 0] * image_grids[:, :, 1]
    slot_ids = jnp.arange(block_total, dtype=jnp.int32)
    own_routing = lax.dynamic_index_in_dim(routing, own_index, 0, keepdims=False)
    seq_rows = text_embeds.shape[0]
    image_rows = jnp.zeros((seq_rows, feature_width), jnp.bfloat16)
    filled_rows = jnp.zeros((), jnp.int32)
    zero_index = jnp.zeros((), jnp.int32)
    for stride in range(block_total):
        own_block = jnp.sum(jnp.where(own_routing == stride, slot_ids, 0))
        outgoing = lax.dynamic_index_in_dim(block_rows, own_block, 0, keepdims=False)
        if stride > 0:
            incoming = passed_along(outgoing, "dp", stride)
        else:
            incoming = outgoing
        source_shard = (own_index - stride) % shard_count
        source_routing = lax.dynamic_index_in_dim(routing, source_shard, 0, keepdims=False)
        source_block = jnp.sum(jnp.where(source_routing == stride, slot_ids, 0))
        source_counts = lax.dynamic_index_in_dim(counts_all, source_shard, 0, keepdims=False)
        image_count = lax.dynamic_index_in_dim(source_counts, source_block, 0, keepdims=False)
        image_rows = lax.dynamic_update_slice(image_rows, incoming, (filled_rows, zero_index))
        filled_rows = filled_rows + image_count
    position = jnp.arange(seq_rows, dtype=jnp.int32)[:, None]
    embeddings = jnp.where(position < filled_rows, image_rows, text_embeds)
    embed_values = embeddings.astype(jnp.float32)
    square_total = lax.psum(jnp.sum(embed_values * embed_values, axis=-1), "tensor")
    scale_rows = lax.rsqrt(square_total / D + 1e-06)
    normed = (embed_values * scale_rows[:, None] * final_gain).astype(jnp.bfloat16)
    return (embeddings, normed)


def solution(mesh):
    placed = (
        P("dp", None),
        P(),
        P(),
        P(None, "tensor"),
        P("tensor"),
        P("tensor", "dp"),
        P("tensor"),
        P("dp", "tensor"),
        P("tensor"),
        P(),
        P(),
    )
    return jax.shard_map(
        per_device,
        mesh=mesh,
        in_specs=placed,
        out_specs=(P("dp", "tensor"), P("dp", "tensor")),
        check_vma=False,
    )
```

profile of v0, /device:TPU:0, one launch (start us, length us, event | category | flops | bytes accessed | tf_op | source)
XLA Modules:
  0.0 334.0 jit_solution(4629358095571909499)
XLA Ops:
  7.2 2.3 convert_reduce_fusion
  9.9 0.8 fusion.2
  10.8 2.5 fusion.5
  13.3 5.2 %convert_element_type.31 = bf16[256,5120]{1,0:T(8,128)(2,1)} reshape(bf16[1024,1280]{1,0:T(8,128)(2,1)} %fusion.5) | data formatting | bytes 5242880 | tf_op jit(solution)/shard_map/convert_element_type | solution.py:32
  18.5 12.5 %fusion.11 = bf16[256,1280]{1,0:T(8,128)(2,1)} fusion(bf16[256,5120]{1,0:T(8,128)(2,1)} %convert_element_type.31, bf16[5120,1280]{1,0:T(8,128)(2,1)} %param.14, f32[1280]{0:T(1024)S(1)} %copy-done.8), kind=kOutput, calls=%fused_computation.20 | convolution fusion | flops 3377070080 | bytes 16389120 | tf_op jit(solution)/shard_map/dot_general | solution.py:34
  31.1 88.7 %all-gather.2.cloned.1.call-done = bf16[2048,1280]{1,0:T(8,128)(2,1)} async-done(((bf16[256,1280]{1,0:T(8,128)(2,1)}), bf16[2048,1280]{1,0:T(8,128)(2,1)}) %all-gather.2.cloned.1.call-update) | async-done | bytes 5242896 | tf_op jit(solution)/shard_map/all_gather | solution.py:40
  119.8 9.7 %convolution_convert_fusion = bf16[2048,1024]{1,0:T(8,128)(2,1)} fusion(bf16[2048,1280]{1,0:T(8,128)(2,1)} %all-gather.2.cloned.1.call-done, bf16[1280,1024]{1,0:T(8,128)(2,1)S(1)} %copy-done), kind=kOutput, calls=%fused_computation.13 | convolution fusion | flops 5370806272 | bytes 12058624 | tf_op jit(solution)/shard_map/dot_general | solution.py:39
  129.5 6.4 %copy.18 = bf16[8,256,1024]{1,2,0:T(8,128)(2,1)} copy(bf16[8,256,1024]{2,1,0:T(8,128)(2,1)} %bitcast.23) | data formatting | bytes 8388608 | tf_op jit(solution)/shard_map/all_to_all | solution.py:44
  136.0 96.4 %all_to_all.19 = bf16[8,256,1024]{1,2,0:T(8,128)(2,1)} all-to-all(bf16[8,256,1024]{1,2,0:T(8,128)(2,1)} %copy.18), channel_id=1, replica_groups=mesh['dp'=8,'tensor'=4] {'dp'}, dimensions={0} | all-to-all | bytes 8388608 | tf_op jit(solution)/shard_map/all_to_all | solution.py:44
  251.3 24.8 %reduce-scatter.2.cloned.1.call-done = bf16[256,2048]{0,1:T(8,128)(2,1)} async-done(((bf16[256,8192]{0,1:T(8,128)(2,1)}), bf16[256,2048]{0,1:T(8,128)(2,1)}) %reduce-scatter.2.cloned.1.call-update) | async-done | bytes 1048592 | tf_op jit(solution)/shard_map/reduce_scatter | solution.py:46
  276.1 2.5 add_convert_fusion
  278.6 2.3 copy.19
  280.9 2.0 dynamic-slice_bitcast_fusion
  282.9 1.4 collective-permute-start
  284.3 1.5 collective-permute-start.1
  285.8 2.4 collective-permute-start.2
  293.1 1.6 dynamic_update_slice.12
  295.2 2.8 dynamic_update_slice.13
  298.0 2.8 dynamic_update_slice.14
  300.8 9.9 %collective-permute-done.2 = bf16[64,2048]{1,0:T(8,128)(2,1)} collective-permute-done((bf16[64,2048]{1,0:T(8,128)(2,1)S(1)}, bf16[64,2048]{1,0:T(8,128)(2,1)}, u32[]{:S(2)}, u32[]{:S(2)}) %collective-permute-start.2) | collective-permute-done | bytes 262176 | tf_op jit(solution)/shard_map/ppermute | solution.py:12
  310.6 2.8 dynamic_update_slice.15
  313.4 4.4 %fusion.6 = (f32[512]{0:T(512)S(1)}, bf16[512,2048]{1,0:T(8,128)(2,1)}) fusion(bf16[512,2048]{1,0:T(8,128)(2,1)} %dynamic_update_slice.15, bf16[512,2048]{1,0:T(8,128)(2,1)} %param.18, pred[512]{0:T(512)(128)(4,1)S(1)} %iota_compare_fusion), kind=kLoop, calls=%fused_computation.10 | loop fusion | flops 4193792 | bytes 6294016 | tf_op jit(solution)/shard_map/reduce_sum | solution.py:78
  317.8 5.9 %psum.7 = f32[512]{0:T(512)S(1)} all-reduce(f32[512]{0:T(512)S(1)} %get-tuple-element.10), channel_id=1, replica_groups=mesh['dp'=8,'tensor'=4] {'tensor'}, use_global_device_ids=true, to_apply=%region_12.13 | all-reduce | flops 512 | bytes 4096 | tf_op jit(solution)/shard_map/psum | solution.py:78
  323.7 3.5 %fusion.8 = bf16[512,2048]{1,0:T(8,128)(2,1)} fusion(bf16[512,2048]{1,0:T(8,128)(2,1)} %get-tuple-element.11, f32[2048]{0:T(1024)S(1)} %copy-done.6, f32[512]{0:T(512)S(1)} %add_rsqrt_fusion.1), kind=kLoop, calls=%fused_computation.12 | loop fusion | flops 4194304 | bytes 4204544 | tf_op jit(solution)/shard_map/convert_element_type | solution.py:80
  (35 shorter events, 5.3 us)
Async XLA Ops:
  7.2 112.7 %copy-start = (bf16[1280,1024]{1,0:T(8,128)(2,1)S(1)}, bf16[1280,1024]{1,0:T(8,128)(2,1)}, u32[]{:S(2)}) copy-start(bf16[1280,1024]{1,0:T(8,128)(2,1)} %param.16) | copy-start | bytes 7864324
  7.2 112.7 %all-gather.2.cloned.1.call-start = ((), (), s32[]{:S(2)}) async-start(), calls=%async_computation.2 | async-start | bytes 5898240 | tf_op jit(solution)/shard_map/all_gather | solution.py:40
  7.2 2.7 copy-start.1
  9.9 0.8 copy-start.3
  9.9 0.8 copy-start.4
  13.3 5.3 %copy-start.8 = (f32[1280]{0:T(1024)S(1)}, f32[1280]{0:T(1024)}, u32[]{:S(2)}) copy-start(f32[1280]{0:T(1024)} %param.15) | copy-start | bytes 15364
  31.1 245.0 %reduce-scatter.2.cloned.1.call-start = ((), (), s32[]{:S(2)}) async-start(), calls=%async_computation.3 | async-start | bytes 5242880 | tf_op jit(solution)/shard_map/reduce_scatter | solution.py:46
  232.4 0.7 copy-start.2
  232.4 43.7 %copy-start.5 = (f32[2048]{0:T(1024)S(1)}, f32[2048]{0:T(1024)}, u32[]{:S(2)}) copy-start(f32[2048]{0:T(1024)} %param.17) | copy-start | bytes 24580
  280.9 7.3 %copy-start.7 = (s32[8,4,2]{0,2,1:T(2,128)S(1)}, s32[8,4,2]{0,2,1:T(2,128)}, u32[]{:S(2)}) copy-start(s32[8,4,2]{0,2,1:T(2,128)} %param.20) | copy-start | bytes 772
  282.9 12.3 %collective-permute-start = (bf16[64,2048]{1,0:T(8,128)(2,1)}, bf16[64,2048]{1,0:T(8,128)(2,1)}, u32[]{:S(2)}, u32[]{:S(2)}) collective-permute-start(bf16[64,2048]{1,0:T(8,128)(2,1)} %get-tuple-element.14), channel_id=1, source_target_pairs={{28,0},{0,4},{4,8},{8,12},{12,16},{16,20},{20,24},{24,28},{29,1},{... | collective-permute-start | bytes 786440 | tf_op jit(solution)/shard_map/ppermute | solution.py:12
  284.3 13.7 %collective-permute-start.1 = (bf16[64,2048]{1,0:T(8,128)(2,1)S(1)}, bf16[64,2048]{1,0:T(8,128)(2,1)}, u32[]{:S(2)}, u32[]{:S(2)}) collective-permute-start(bf16[64,2048]{1,0:T(8,128)(2,1)S(1)} %get-tuple-element.13), channel_id=1, source_target_pairs={{24,0},{28,4},{0,8},{4,12},{8,16},{12,20},{16,24},{20,28},{25,1},{... | collective-permute-start | bytes 786440 | tf_op jit(solution)/shard_map/ppermute | solution.py:12
  285.8 24.8 %collective-permute-start.2 = (bf16[64,2048]{1,0:T(8,128)(2,1)S(1)}, bf16[64,2048]{1,0:T(8,128)(2,1)}, u32[]{:S(2)}, u32[]{:S(2)}) collective-permute-start(bf16[64,2048]{1,0:T(8,128)(2,1)S(1)} %get-tuple-element.12), channel_id=1, source_target_pairs={{20,0},{24,4},{28,8},{0,12},{4,16},{8,20},{12,24},{16,28},{21,1},{... | collective-permute-start | bytes 786440 | tf_op jit(solution)/shard_map/ppermute | solution.py:12
  313.4 10.2 %copy-start.6 = (f32[2048]{0:T(1024)S(1)}, f32[2048]{0:T(1024)}, u32[]{:S(2)}) copy-start(f32[2048]{0:T(1024)} %param.19) | copy-start | bytes 24580
Sparse Core Ops, SparseCore 0:
  31.2 88.5 all-gather.1
  232.5 43.5 reduce-scatter.1
where the time goes:
time: 335 us; the launch traced here: 334 us
  waiting for transfers between devices  124 us (37%)
  blocking collectives  102 us (30%)
  between operations  33.7 us (10%)
  local copies, waits for them, and re-layouts  27.5 us (8%)
  matrix products  22.2 us (7%)
  other arithmetic  19.1 us (6%)
  starting transfers between devices  5.41 us (2%)
    all_to_all x1, blocking collectives, per_device(): lax.all_to_all(partial_value, 'dp', split_axis=0, concat_axis=1, tiled=True)  96.4 us
    all_gather x1, waiting for transfers between devices, per_device(): lax.all_gather(hidden, 'dp', axis=0, tiled=True)  88.7 us
    reduce_scatter x1, waiting for transfers between devices, per_device(): lax.psum_scatter(partial_terms.astype(jnp.bfloat16), 'tensor', scatter_di...  24.8 us
    dot_general x1, matrix products, per_device(): jnp.dot(merged, first_weight, preferred_element_type=jnp.float32)  12.5 us
    ppermute x3, waiting for transfers between devices, passed_along(): return lax.ppermute(block, axis, route)  10.3 us
    dynamic_update_slice x4, local copies, waits for them, and re-layouts, per_device(): lax.dynamic_update_slice(image_rows, incoming, (filled_rows, zero_index))  9.95 us
    dot_general x1, matrix products, per_device(): jnp.dot(lax.all_gather(hidden, 'dp', axis=0, tiled=True), second_weight,...  9.71 us
  transfers between devices with their start and end apart: 5, of which 4 were waited for; matrix products, arithmetic and copies ran while one was open for 3% of the time, Pallas kernels for 0%

commit v1 on v0

--- a/solution.py
+++ b/solution.py
@@ -1,9 +1,25 @@
+import functools
 import jax
 import jax.numpy as jnp
 from jax import lax
 from jax.sharding import PartitionSpec as P
 
 D = 8192
+
+
+def map_clusters(unit, net_axis, dim_at, array_axis):
+    return jnp.concatenate(
+        lax.all_to_all(
+            jnp.stack(jnp.split(unit, lax.axis_size(net_axis), axis=dim_at), axis=0),
+            axis_name=net_axis,
+            split_axis=0,
+            concat_axis=0,
+        ),
+        axis=array_axis,
+    )
+
+
+arrange_cubes = functools.partial(map_clusters, net_axis="dp", dim_at=0, array_axis=1)
 
 
 def passed_along(block, axis, distance):
@@ -41,7 +57,7 @@
         second_weight,
         preferred_element_type=jnp.float32,
     ).astype(jnp.bfloat16)
-    columns = lax.all_to_all(partial_value, "dp", split_axis=0, concat_axis=1, tiled=True)
+    columns = arrange_cubes(partial_value)
     partial_terms = columns.astype(jnp.float32)
     summed = lax.psum_scatter(
         partial_terms.astype(jnp.bfloat16), "tensor", scatter_dimension=1, tiled=True

time: 335 us -> 333 us (level)
    all_to_all x1 -> x0, local copies, waits for them, and re-layouts: 6.45 us -> none  [per_device(): lax.all_to_all(partial_value, 'dp', split_axis=0, concat_axis=1, tiled=True)]
    reshape x0 -> x1, local copies, waits for them, and re-layouts: none -> 6.43 us  [map_clusters(): jnp.concatenate(lax.all_to_all(jnp.stack(jnp.split(unit, lax.axis_size(ne...]
where the time goes in v1:
time: 333 us; the launch traced here: 332 us
  waiting for transfers between devices  124 us (37%)
  blocking collectives  102 us (31%)
  between operations  33.7 us (10%)
  local copies, waits for them, and re-layouts  27.8 us (8%)
  matrix products  20.8 us (6%)
  other arithmetic  19.1 us (6%)
  starting transfers between devices  5.46 us (2%)
    all_to_all x1, blocking collectives, map_clusters(): lax.all_to_all(jnp.stack(jnp.split(unit, lax.axis_size(net_axis), axis=di...  96.1 us
    all_gather x1, waiting for transfers between devices, per_device(): lax.all_gather(hidden, 'dp', axis=0, tiled=True)  88.7 us
    reduce_scatter x1, waiting for transfers between devices, per_device(): lax.psum_scatter(partial_terms.astype(jnp.bfloat16), 'tensor', scatter_di...  24.6 us
    dot_general x1, matrix products, per_device(): jnp.dot(merged, first_weight, preferred_element_type=jnp.float32)  12.5 us
    ppermute x3, waiting for transfers between devices, passed_along(): return lax.ppermute(block, axis, route)  10.3 us
    dynamic_update_slice x4, local copies, waits for them, and re-layouts, per_device(): lax.dynamic_update_slice(image_rows, incoming, (filled_rows, zero_index))  9.95 us
    dot_general x1, matrix products, per_device(): jnp.dot(lax.all_gather(hidden, 'dp', axis=0, tiled=True), second_weight,...  8.3 us
  transfers between devices with their start and end apart: 5, of which 4 were waited for; matrix products, arithmetic and copies ran while one was open for 3% of the time, Pallas kernels for 0%

profile of v1, /device:TPU:0, one launch (start us, length us, event | category | flops | bytes accessed | tf_op | source)
XLA Modules:
  0.0 332.5 jit_solution(9564299911129974610)
XLA Ops:
  7.3 2.3 convert_reduce_fusion
  9.9 0.8 fusion.2
  10.8 2.5 fusion.5
  13.3 5.2 %convert_element_type.31 = bf16[256,5120]{1,0:T(8,128)(2,1)} reshape(bf16[1024,1280]{1,0:T(8,128)(2,1)} %fusion.5) | data formatting | bytes 5242880 | tf_op jit(solution)/shard_map/convert_element_type | solution.py:48
  18.5 12.5 %fusion.11 = bf16[256,1280]{1,0:T(8,128)(2,1)} fusion(bf16[256,5120]{1,0:T(8,128)(2,1)} %convert_element_type.31, bf16[5120,1280]{1,0:T(8,128)(2,1)} %param.14, f32[1280]{0:T(1024)S(1)} %copy-done.8), kind=kOutput, calls=%fused_computation.20 | convolution fusion | flops 3377070080 | bytes 16389120 | tf_op jit(solution)/shard_map/dot_general | solution.py:50
  31.1 88.7 %all-gather.2.cloned.1.call-done = bf16[2048,1280]{1,0:T(8,128)(2,1)} async-done(((bf16[256,1280]{1,0:T(8,128)(2,1)}), bf16[2048,1280]{1,0:T(8,128)(2,1)}) %all-gather.2.cloned.1.call-update) | async-done | bytes 5242896 | tf_op jit(solution)/shard_map/all_gather | solution.py:56
  119.8 8.3 %convolution_convert_fusion = bf16[2048,1024]{1,0:T(8,128)(2,1)S(1)} fusion(bf16[2048,1280]{1,0:T(8,128)(2,1)} %all-gather.2.cloned.1.call-done, bf16[1280,1024]{1,0:T(8,128)(2,1)S(1)} %copy-done), kind=kOutput, calls=%fused_computation.13 | convolution fusion | flops 5370806272 | bytes 12058624 | tf_op jit(solution)/shard_map/dot_general | solution.py:55
  128.5 96.1 %all_to_all.5 = bf16[8,256,1024]{2,1,0:T(8,128)(2,1)} all-to-all(bf16[8,256,1024]{2,1,0:T(8,128)(2,1)S(1)} %fusion.19), channel_id=1, replica_groups=mesh['dp'=8,'tensor'=4] {'dp'}, dimensions={0} | all-to-all | bytes 8388608 | tf_op jit(solution)/shard_map/all_to_all | solution.py:12
  224.6 6.4 %copy.18 = bf16[256,8,1024]{0,2,1:T(8,128)(2,1)} copy(bf16[256,8,1024]{2,0,1:T(8,128)(2,1)} %bitcast.52) | data formatting | bytes 8388608 | tf_op jit(solution)/shard_map/reshape | solution.py:11
  250.0 24.6 %reduce-scatter.2.cloned.1.call-done = bf16[256,2048]{0,1:T(8,128)(2,1)} async-done(((bf16[256,8192]{0,1:T(8,128)(2,1)}), bf16[256,2048]{0,1:T(8,128)(2,1)}) %reduce-scatter.2.cloned.1.call-update) | async-done | bytes 1048592 | tf_op jit(solution)/shard_map/reduce_scatter | solution.py:62
  274.6 2.5 add_convert_fusion
  277.1 2.3 copy.19
  279.4 2.0 dynamic-slice_bitcast_fusion
  281.3 1.5 collective-permute-start
  282.8 1.5 collective-permute-start.1
  284.3 2.4 collective-permute-start.2
  291.7 1.6 dynamic_update_slice.12
  293.6 2.8 dynamic_update_slice.13
  296.4 2.8 dynamic_update_slice.14
  299.2 9.9 %collective-permute-done.2 = bf16[64,2048]{1,0:T(8,128)(2,1)} collective-permute-done((bf16[64,2048]{1,0:T(8,128)(2,1)S(1)}, bf16[64,2048]{1,0:T(8,128)(2,1)}, u32[]{:S(2)}, u32[]{:S(2)}) %collective-permute-start.2) | collective-permute-done | bytes 262176 | tf_op jit(solution)/shard_map/ppermute | solution.py:28
  309.1 2.8 dynamic_update_slice.15
  311.9 4.4 %fusion.6 = (f32[512]{0:T(512)S(1)}, bf16[512,2048]{1,0:T(8,128)(2,1)}) fusion(bf16[512,2048]{1,0:T(8,128)(2,1)} %dynamic_update_slice.15, bf16[512,2048]{1,0:T(8,128)(2,1)} %param.18, pred[512]{0:T(512)(128)(4,1)S(1)} %iota_compare_fusion), kind=kLoop, calls=%fused_computation.10 | loop fusion | flops 4193792 | bytes 6294016 | tf_op jit(solution)/shard_map/reduce_sum | solution.py:94
  316.3 5.9 %psum.7 = f32[512]{0:T(512)S(1)} all-reduce(f32[512]{0:T(512)S(1)} %get-tuple-element.10), channel_id=1, replica_groups=mesh['dp'=8,'tensor'=4] {'tensor'}, use_global_device_ids=true, to_apply=%region_12.13 | all-reduce | flops 512 | bytes 4096 | tf_op jit(solution)/shard_map/psum | solution.py:94
  322.2 3.5 %fusion.8 = bf16[512,2048]{1,0:T(8,128)(2,1)} fusion(bf16[512,2048]{1,0:T(8,128)(2,1)} %get-tuple-element.11, f32[2048]{0:T(1024)S(1)} %copy-done.6, f32[512]{0:T(512)S(1)} %add_rsqrt_fusion.1), kind=kLoop, calls=%fused_computation.12 | loop fusion | flops 4194304 | bytes 4204544 | tf_op jit(solution)/shard_map/convert_element_type | solution.py:96
  (43 shorter events, 5.5 us)
Async XLA Ops:
  7.2 112.7 %copy-start = (bf16[1280,1024]{1,0:T(8,128)(2,1)S(1)}, bf16[1280,1024]{1,0:T(8,128)(2,1)}, u32[]{:S(2)}) copy-start(bf16[1280,1024]{1,0:T(8,128)(2,1)} %param.16) | copy-start | bytes 7864324
  7.2 3.6 %copy-start.3 = (f32[1280]{0:T(1024)S(1)}, f32[1280]{0:T(1024)}, u32[]{:S(2)}) copy-start(f32[1280]{0:T(1024)} %param.13) | copy-start | bytes 15364
  7.2 112.6 %all-gather.2.cloned.1.call-start = ((), (), s32[]{:S(2)}) async-start(), calls=%async_computation.2 | async-start | bytes 5898240 | tf_op jit(solution)/shard_map/all_gather | solution.py:56
  7.2 2.7 copy-start.1
  7.2 3.5 %copy-start.4 = (f32[1280]{0:T(1024)S(1)}, f32[1280]{0:T(1024)}, u32[]{:S(2)}) copy-start(f32[1280]{0:T(1024)} %param.12) | copy-start | bytes 15364
  13.3 5.3 %copy-start.8 = (f32[1280]{0:T(1024)S(1)}, f32[1280]{0:T(1024)}, u32[]{:S(2)}) copy-start(f32[1280]{0:T(1024)} %param.15) | copy-start | bytes 15364
  31.1 243.5 %reduce-scatter.2.cloned.1.call-start = ((), (), s32[]{:S(2)}) async-start(), calls=%async_computation.3 | async-start | bytes 5242880 | tf_op jit(solution)/shard_map/reduce_scatter | solution.py:62
  231.1 0.7 copy-start.2
  231.1 43.5 %copy-start.5 = (f32[2048]{0:T(1024)S(1)}, f32[2048]{0:T(1024)}, u32[]{:S(2)}) copy-start(f32[2048]{0:T(1024)} %param.17) | copy-start | bytes 24580
  277.1 9.6 %copy-start.7 = (s32[8,4,2]{0,2,1:T(2,128)S(1)}, s32[8,4,2]{0,2,1:T(2,128)}, u32[]{:S(2)}) copy-start(s32[8,4,2]{0,2,1:T(2,128)} %param.20) | copy-start | bytes 772
  281.3 12.3 %collective-permute-start = (bf16[64,2048]{1,0:T(8,128)(2,1)}, bf16[64,2048]{1,0:T(8,128)(2,1)}, u32[]{:S(2)}, u32[]{:S(2)}) collective-permute-start(bf16[64,2048]{1,0:T(8,128)(2,1)} %get-tuple-element.14), channel_id=1, source_target_pairs={{28,0},{0,4},{4,8},{8,12},{12,16},{16,20},{20,24},{24,28},{29,1},{... | collective-permute-start | bytes 786440 | tf_op jit(solution)/shard_map/ppermute | solution.py:28
  282.8 13.6 %collective-permute-start.1 = (bf16[64,2048]{1,0:T(8,128)(2,1)S(1)}, bf16[64,2048]{1,0:T(8,128)(2,1)}, u32[]{:S(2)}, u32[]{:S(2)}) collective-permute-start(bf16[64,2048]{1,0:T(8,128)(2,1)S(1)} %get-tuple-element.13), channel_id=1, source_target_pairs={{24,0},{28,4},{0,8},{4,12},{8,16},{12,20},{16,24},{20,28},{25,1},{... | collective-permute-start | bytes 786440 | tf_op jit(solution)/shard_map/ppermute | solution.py:28
  284.3 24.8 %collective-permute-start.2 = (bf16[64,2048]{1,0:T(8,128)(2,1)S(1)}, bf16[64,2048]{1,0:T(8,128)(2,1)}, u32[]{:S(2)}, u32[]{:S(2)}) collective-permute-start(bf16[64,2048]{1,0:T(8,128)(2,1)S(1)} %get-tuple-element.12), channel_id=1, source_target_pairs={{20,0},{24,4},{28,8},{0,12},{4,16},{8,20},{12,24},{16,28},{21,1},{... | collective-permute-start | bytes 786440 | tf_op jit(solution)/shard_map/ppermute | solution.py:28
  311.9 10.3 %copy-start.6 = (f32[2048]{0:T(1024)S(1)}, f32[2048]{0:T(1024)}, u32[]{:S(2)}) copy-start(f32[2048]{0:T(1024)} %param.19) | copy-start | bytes 24580
Sparse Core Ops, SparseCore 0:
  31.2 88.5 all-gather.1
  231.2 43.2 reduce-scatter.1
